TPU v7x, 32 devices: a whole 2x2x4 slice. The times are simulated.
32 devices in a mesh: ka: 8 (over z, y), ga: 4 (over x, core).
Axes of the slice: x: 2, y: 2, z: 4, core: 2. Of those that a mesh axis runs over, the one named last changes fastest.
Arguments:
- x_dens: bfloat16 [32, 64, 1500], P('ka', None, 'ga'), may hold values from -6 to 6
- y_dens: bfloat16 [32, 64, 1500], P('ka', None, 'ga'), may hold values from -0.15625 to 0.15625
- p_dens: bfloat16 [32, 64, 1500], P('ka', None, 'ga'), may hold values from -1 to 1
- coulomb: float32 [1500], P('ga'), may hold values from 0.1 to 2
- screened: bfloat16 [16, 1500, 1500], P('ka', 'ga'), may hold values from -0.15625 to 0.15625
- pairs: int32 [128, 3], P('ka'), may hold values from 0 to 31, as said below
- q_slot: int32 [16], replicated, may hold values from 0 to 15, as said below
Outputs:
- blocks: float32 [128, 4096], P('ka')
- mirrored: float32 [32, 4096], P('ka')
Inputs may be any that keep to these rules, and one draw needn't show every extreme that they name: `pairs`: column 0 of the rows held by index d of ka lies in d * 4 to (d + 1) * 4 - 1; column 1 is any k-point; column 2 is a momentum transfer below 16. Among one index's 16 rows at most 2 have a second k-point held by one same index, and this is reached; at most 2 have q_slot[q] // 2 equal to one same value, and this is reached. `q_slot`: A permutation of the slots; slot s of screened is held by index s // 2 of ka.
All inputs are finite; a program needn't handle non-finite values.
Results may differ from a plain program's by a relative error of at most 0.0014.
Values may be sent and summed in bfloat16 or wider, within the bound.
A program may use at most 192 MiB of HBM per device.

v0:
```python
import jax
import jax.numpy as jnp
from jax import lax
from jax.sharding import PartitionSpec as P

CAPQ = 2
CAPK = 2


def earlier_count(owners):
    places = jnp.arange(owners.shape[0])
    same_owner = owners[:, None] == owners[None, :]
    before = places[:, None] > places[None, :]
    return jnp.sum(jnp.logical_and(same_owner, before).astype(jnp.int32), axis=1)


def per_device(x_dens, y_dens, p_dens, coulomb, screened, pairs, q_slot):
    n_ka = lax.axis_size("ka")
    mine_index = lax.axis_index("ka")
    per_dev, transitions, g_local = x_dens.shape
    q_slots = screened.shape[0]
    pair_rows = pairs.shape[0]
    k_local = pairs[:, 0] - mine_index * per_dev
    partner = pairs[:, 1]
    q_index = pairs[:, 2]
    slot_of = jnp.sum(
        jnp.where(q_index[:, None] == jnp.arange(q_slot.shape[0])[None, :], q_slot[None, :], 0),
        axis=1,
    )
    q_owner = slot_of // q_slots
    q_local = slot_of % q_slots
    q_rank = earlier_count(q_owner)
    q_route = ((q_owner * CAPQ + q_rank)[:, None] == jnp.arange(n_ka * CAPQ)[None, :]).astype(
        jnp.bfloat16
    )
    pick_first = (k_local[:, None] == jnp.arange(per_dev)[None, :]).astype(jnp.bfloat16)
    x_rows = jnp.einsum(
        "jk,kig->jig", pick_first, x_dens, preferred_element_type=jnp.float32
    ).astype(jnp.bfloat16)
    p_rows = jnp.einsum(
        "jk,kig->jig", pick_first, p_dens, preferred_element_type=jnp.float32
    ).astype(jnp.bfloat16)
    send_x = jnp.einsum("js,jig->sig", q_route, x_rows, preferred_element_type=jnp.float32).astype(
        jnp.bfloat16
    )
    send_x = send_x.reshape(n_ka, CAPQ, transitions, g_local)
    send_q = jnp.sum(q_route.astype(jnp.int32) * q_local[:, None], axis=0).reshape(n_ka, CAPQ)
    got_x, got_q = (
        lax.all_to_all(send_x, "ka", split_axis=0, concat_axis=0, tiled=True),
        lax.all_to_all(send_q, "ka", split_axis=0, concat_axis=0, tiled=True),
    )
    chosen = (got_q[:, :, None] == jnp.arange(q_slots)[None, None, :]).astype(jnp.bfloat16)
    stacked = got_x[:, :, None, :, :] * chosen[:, :, :, None, None]
    partial_value = jnp.einsum(
        "ncsig,sgh->hnci", stacked, screened, preferred_element_type=jnp.float32
    )
    half_rows = lax.psum_scatter(
        partial_value.reshape(lax.axis_size("ga") * g_local, n_ka, CAPQ * transitions),
        "ga",
        scatter_dimension=0,
        tiled=True,
    ).astype(jnp.bfloat16)
    returned = lax.all_to_all(half_rows, "ka", split_axis=1, concat_axis=1, tiled=True)
    returned = returned.reshape(g_local, n_ka * CAPQ, transitions)
    u_rows = jnp.einsum(
        "js,gsi->jig", q_route, returned, preferred_element_type=jnp.float32
    ).astype(jnp.bfloat16)
    all_pairs = lax.all_gather(pairs, "ka", axis=0, tiled=True).reshape(n_ka, pair_rows, 3)
    seconds = all_pairs[:, :, 1]
    k_owners = seconds // per_dev
    k_ranks = jax.vmap(earlier_count)(k_owners)
    held_here = k_owners == mine_index
    rank_hot = (k_ranks[:, :, None] == jnp.arange(CAPK)[None, None, :]).astype(jnp.float32)
    local_hot = jnp.logical_and(
        (seconds - mine_index * per_dev)[:, :, None] == jnp.arange(per_dev)[None, None, :],
        held_here[:, :, None],
    ).astype(jnp.float32)
    selector = jnp.einsum("njc,njk->nck", rank_hot, local_hot).astype(jnp.bfloat16)
    send_y = jnp.einsum(
        "nck,kig->ncig", selector, y_dens, preferred_element_type=jnp.float32
    ).astype(jnp.bfloat16)
    send_p = jnp.einsum(
        "nck,kig->ncig", selector, p_dens, preferred_element_type=jnp.float32
    ).astype(jnp.bfloat16)
    got_y, got_p = (
        lax.all_to_all(send_y, "ka", split_axis=0, concat_axis=0, tiled=True),
        lax.all_to_all(send_p, "ka", split_axis=0, concat_axis=0, tiled=True),
    )
    own_rank = earlier_count(partner // per_dev)
    pick_second = (
        (partner // per_dev * CAPK + own_rank)[:, None] == jnp.arange(n_ka * CAPK)[None, :]
    ).astype(jnp.bfloat16)
    y_rows = jnp.einsum(
        "js,sig->jig",
        pick_second,
        got_y.reshape(n_ka * CAPK, transitions, g_local),
        preferred_element_type=jnp.float32,
    ).astype(jnp.bfloat16)
    pp_rows = jnp.einsum(
        "js,sig->jig",
        pick_second,
        got_p.reshape(n_ka * CAPK, transitions, g_local),
        preferred_element_type=jnp.float32,
    ).astype(jnp.bfloat16)
    direct = jnp.einsum("jig,jhg->jih", u_rows, y_rows, preferred_element_type=jnp.float32)
    weighted = p_rows.astype(jnp.float32) * coulomb[None, None, :]
    exchange_term = jnp.einsum(
        "jig,jhg->jih", weighted, pp_rows.astype(jnp.float32), precision=lax.Precision.HIGHEST
    )
    kernel_block = lax.psum(2.0 * exchange_term - direct, "ga")
    blocks = kernel_block.reshape(pair_rows, transitions * transitions)
    flipped = jnp.transpose(kernel_block, (0, 2, 1)).reshape(pair_rows, transitions * transitions)
    selector = (partner[:, None] == jnp.arange(lax.axis_size("ka") * per_dev)[None, :]).astype(
        jnp.float32
    )
    mirrored = lax.psum_scatter(
        jnp.dot(selector.T, flipped, precision=lax.Precision.HIGHEST),
        "ka",
        scatter_dimension=0,
        tiled=True,
    )
    return (blocks, mirrored)


def solution(mesh):
    in_specs = (
        P("ka", None, "ga"),
        P("ka", None, "ga"),
        P("ka", None, "ga"),
        P("ga"),
        P("ka", "ga", None),
        P("ka", None),
        P(),
    )
    out_specs = (P("ka", None), P("ka", None))
    return jax.shard_map(
        per_device, mesh=mesh, in_specs=in_specs, out_specs=out_specs, check_vma=False
    )
```

profile of v0, /device:TPU:0, one launch (start us, length us, event | category | flops | bytes accessed | tf_op | source)
XLA Modules:
  0.0 274.0 jit_solution(15575906817718074861)
XLA Ops:
  9.9 7.3 %all-to-all-start.2 = ((s32[8,1,2]{2,1,0:T(1,128)}), s32[8,1,2]{2,1,0:T(1,128)S(1)}, u32[]{:S(2)}, u32[]{:S(2)}) async-start(s32[8,1,2]{2,1,0:T(1,128)} %bitcast.18), calls=%async_computation.2 | async-start | bytes 8192 | tf_op jit(solution)/shard_map/all_to_all | solution.py:50
  17.2 2.5 convolution_convert_fusion.3
  19.7 2.2 reshape.166
  21.9 1.5 copy.117
  23.6 5.8 %all-to-all-start.1 = ((bf16[8,2,64,375]{3,1,2,0:T(2,128)(2,1)}), bf16[8,2,64,375]{3,1,2,0:T(2,128)(2,1)S(1)}, u32[]{:S(2)}, u32[]{:S(2)}) async-start(bf16[8,2,64,375]{3,1,2,0:T(2,128)(2,1)} %copy.117), calls=%async_computation.1 | async-start | bytes 1572864 | tf_op jit(solution)/shard_map/all_to_all | solution.py:49
  29.5 19.6 %all-to-all-done.1 = bf16[8,2,64,375]{3,1,2,0:T(2,128)(2,1)S(1)} async-done(((bf16[8,2,64,375]{3,1,2,0:T(2,128)(2,1)}), bf16[8,2,64,375]{3,1,2,0:T(2,128)(2,1)S(1)}, u32[]{:S(2)}, u32[]{:S(2)}) %all-to-all-start.1) | async-done | bytes 768032 | tf_op jit(solution)/shard_map/all_to_all | solution.py:49
  49.2 5.0 %fusion = f32[8,2,64,1500,1]{3,2,4,1,0:T(8,128)} fusion(bf16[2,375,1500,1,1]{2,0,1,4,3:T(2,128)(2,1)S(1)} %bitcast.72, bf16[8,2,2]{2,1,0:T(2,128)(2,1)S(1)} %compare_convert_fusion, bf16[8,2,64,375]{3,2,1,0:T(8,128)(2,1)S(1)} %copy.118), kind=kOutput, calls=%fused_computation | convolution fusion | flops 2304768000 | bytes 9162064 | tf_op jit(solution)/shard_map/ncsig,sgh->hnci/dot_general | solution.py:54
  54.2 6.5 %copy.123 = f32[1500,8,128]{2,1,0:T(8,128)} copy(f32[1500,8,128]{0,2,1:T(8,128)} %bitcast.73) | data formatting | bytes 12288000 | tf_op jit(solution)/shard_map/reshape | solution.py:58
  61.4 26.1 %all-gather = s32[8,16,3]{1,2,0:T(4,128)S(1)} all-gather(s32[1,16,3]{1,2,0:T(4,128)S(1)} %bitcast.81), channel_id=1, replica_groups=mesh['ka'=8,'ga'=4] {'ka'}, dimensions={0}, use_global_device_ids=true | all-gather | bytes 1728 | tf_op jit(solution)/shard_map/all_gather | solution.py:68
  89.6 3.5 %all-to-all-start = ((bf16[8,2,64,375]{3,2,1,0:T(8,128)(2,1)}), bf16[8,2,64,375]{3,2,1,0:T(8,128)(2,1)S(1)}, u32[]{:S(2)}, u32[]{:S(2)}) async-start(bf16[8,2,64,375]{3,2,1,0:T(8,128)(2,1)} %copy.111), calls=%async_computation | async-start | bytes 1572864 | tf_op jit(solution)/shard_map/all_to_all | solution.py:87
  94.6 13.4 %all-to-all-done = bf16[8,2,64,375]{3,2,1,0:T(8,128)(2,1)S(1)} async-done(((bf16[8,2,64,375]{3,2,1,0:T(8,128)(2,1)}), bf16[8,2,64,375]{3,2,1,0:T(8,128)(2,1)S(1)}, u32[]{:S(2)}, u32[]{:S(2)}) %all-to-all-start) | async-done | bytes 768032 | tf_op jit(solution)/shard_map/all_to_all | solution.py:87
  108.0 4.2 %all-to-all-start.4 = ((bf16[8,2,64,375]{3,2,1,0:T(8,128)(2,1)}), bf16[8,2,64,375]{3,2,1,0:T(8,128)(2,1)}, u32[]{:S(2)}, u32[]{:S(2)}) async-start(bf16[8,2,64,375]{3,2,1,0:T(8,128)(2,1)} %copy.128), calls=%async_computation.4 | async-start | bytes 1572864 | tf_op jit(solution)/shard_map/all_to_all | solution.py:86
  112.2 5.5 %reduce-scatter.4.cloned.1.call-done = f32[375,8,128]{2,1,0:T(8,128)} async-done(((f32[1500,8,128]{2,1,0:T(8,128)}), f32[375,8,128]{2,1,0:T(8,128)}) %reduce-scatter.4.cloned.1.call-update) | async-done | bytes 1536016
  117.7 1.5 convert_element_type.77
  120.1 9.4 %all-to-all-done.4 = bf16[8,2,64,375]{3,2,1,0:T(8,128)(2,1)} async-done(((bf16[8,2,64,375]{3,2,1,0:T(8,128)(2,1)}), bf16[8,2,64,375]{3,2,1,0:T(8,128)(2,1)}, u32[]{:S(2)}, u32[]{:S(2)}) %all-to-all-start.4) | async-done | bytes 768032 | tf_op jit(solution)/shard_map/all_to_all | solution.py:86
  129.5 4.2 %all-to-all-start.3 = ((bf16[375,8,128]{2,0,1:T(8,128)(2,1)}), bf16[375,8,128]{2,0,1:T(8,128)(2,1)}, u32[]{:S(2)}, u32[]{:S(2)}) async-start(bf16[375,8,128]{2,0,1:T(8,128)(2,1)} %copy.124), calls=%async_computation.3 | async-start | bytes 1540096 | tf_op jit(solution)/shard_map/all_to_all | solution.py:63
  135.0 2.6 convolution_convert_fusion
  137.7 2.3 fusion.6
  140.0 12.0 %all-to-all-done.3 = bf16[375,8,128]{2,0,1:T(8,128)(2,1)} async-done(((bf16[375,8,128]{2,0,1:T(8,128)(2,1)}), bf16[375,8,128]{2,0,1:T(8,128)(2,1)}, u32[]{:S(2)}, u32[]{:S(2)}) %all-to-all-start.3) | async-done | bytes 768032 | tf_op jit(solution)/shard_map/all_to_all | solution.py:63
  152.0 1.5 copy.125
  156.0 32.5 %all-reduce.5.cloned.1.call-done = f32[16,64,64]{2,1,0:T(8,128)} async-done(((f32[16,64,64]{2,1,0:T(8,128)}), f32[16,64,64]{2,1,0:T(8,128)}) %all-reduce.5.cloned.1.call-update) | async-done | bytes 262160 | tf_op jit(solution)/shard_map/psum | solution.py:110
  190.7 2.2 fusion.37
  195.1 70.8 %all-reduce.7.cloned.1.call-done = f32[32,4096]{1,0:T(8,128)} async-done(((f32[32,4096]{1,0:T(8,128)}), f32[32,4096]{1,0:T(8,128)}) %all-reduce.7.cloned.1.call-update) | async-done | bytes 524304
  265.9 1.5 constant_dynamic-slice_fusion
  (58 shorter events, 15.8 us)
Async XLA Ops:
  7.2 42.0 %copy-start = (bf16[2,375,1500]{2,0,1:T(2,128)(2,1)S(1)}, bf16[2,375,1500]{2,0,1:T(2,128)(2,1)}, u32[]{:S(2)}) copy-start(bf16[2,375,1500]{2,0,1:T(2,128)(2,1)} %param.11) | copy-start | bytes 6750004
  9.9 13.7 %all-to-all-start.2 = ((s32[8,1,2]{2,1,0:T(1,128)}), s32[8,1,2]{2,1,0:T(1,128)S(1)}, u32[]{:S(2)}, u32[]{:S(2)}) async-start(s32[8,1,2]{2,1,0:T(1,128)} %bitcast.18), calls=%async_computation.2 | async-start | bytes 8192 | tf_op jit(solution)/shard_map/all_to_all | solution.py:50
  23.6 25.5 %all-to-all-start.1 = ((bf16[8,2,64,375]{3,1,2,0:T(2,128)(2,1)}), bf16[8,2,64,375]{3,1,2,0:T(2,128)(2,1)S(1)}, u32[]{:S(2)}, u32[]{:S(2)}) async-start(bf16[8,2,64,375]{3,1,2,0:T(2,128)(2,1)} %copy.117), calls=%async_computation.1 | async-start | bytes 1572864 | tf_op jit(solution)/shard_map/all_to_all | solution.py:49
  29.4 88.3 %reduce-scatter.4.cloned.1.call-start = ((), (), s32[]{:S(2)}) async-start(), calls=%async_computation.8 | async-start | bytes 7680000
  60.7 0.7 copy-start.6
  60.7 27.4 %copy-start.4 = (bf16[4,64,375]{2,1,0:T(8,128)(2,1)S(1)}, bf16[4,64,375]{2,1,0:T(8,128)(2,1)}, u32[]{:S(2)}) copy-start(bf16[4,64,375]{2,1,0:T(8,128)(2,1)} %param.9) | copy-start | bytes 576004
  88.5 4.6 %copy-start.5 = (bf16[4,64,375]{2,1,0:T(8,128)(2,1)S(1)}, bf16[4,64,375]{2,1,0:T(8,128)(2,1)}, u32[]{:S(2)}) copy-start(bf16[4,64,375]{2,1,0:T(8,128)(2,1)} %param.8) | copy-start | bytes 576004
  89.6 18.4 %all-to-all-start = ((bf16[8,2,64,375]{3,2,1,0:T(8,128)(2,1)}), bf16[8,2,64,375]{3,2,1,0:T(8,128)(2,1)S(1)}, u32[]{:S(2)}, u32[]{:S(2)}) async-start(bf16[8,2,64,375]{3,2,1,0:T(8,128)(2,1)} %copy.111), calls=%async_computation | async-start | bytes 1572864 | tf_op jit(solution)/shard_map/all_to_all | solution.py:87
  108.0 21.6 %all-to-all-start.4 = ((bf16[8,2,64,375]{3,2,1,0:T(8,128)(2,1)}), bf16[8,2,64,375]{3,2,1,0:T(8,128)(2,1)}, u32[]{:S(2)}, u32[]{:S(2)}) async-start(bf16[8,2,64,375]{3,2,1,0:T(8,128)(2,1)} %copy.128), calls=%async_computation.4 | async-start | bytes 1572864 | tf_op jit(solution)/shard_map/all_to_all | solution.py:86
  119.1 14.9 %copy-start.7 = (f32[375]{0:T(512)S(1)}, f32[375]{0:T(512)}, u32[]{:S(2)}) copy-start(f32[375]{0:T(512)} %param.10) | copy-start | bytes 4504
  129.5 22.4 %all-to-all-start.3 = ((bf16[375,8,128]{2,0,1:T(8,128)(2,1)}), bf16[375,8,128]{2,0,1:T(8,128)(2,1)}, u32[]{:S(2)}, u32[]{:S(2)}) async-start(bf16[375,8,128]{2,0,1:T(8,128)(2,1)} %copy.124), calls=%async_computation.3 | async-start | bytes 1540096 | tf_op jit(solution)/shard_map/all_to_all | solution.py:63
  133.7 54.8 %all-reduce.5.cloned.1.call-start = ((), (), s32[]{:S(2)}) async-start(), calls=%async_computation.6 | async-start | bytes 1048576 | tf_op jit(solution)/shard_map/psum | solution.py:110
  153.5 1.1 copy-start.1
  153.5 1.3 copy-start.3
  156.0 109.9 %all-reduce.7.cloned.1.call-start = ((), (), s32[]{:S(2)}) async-start(), calls=%async_computation.7 | async-start | bytes 1048576
  188.5 4.5 %copy-start.8 = (u32[32]{0:T(128)S(1)}, u32[32]{0:T(128)}, u32[]{:S(2)}) copy-start(u32[32]{0:T(128)} %constant.69) | copy-start | bytes 388
  188.5 5.7 %copy-start.2 = (f32[16,64,64]{2,1,0:T(8,128)S(1)}, f32[16,64,64]{2,1,0:T(8,128)}, u32[]{:S(2)}) copy-start(f32[16,64,64]{2,1,0:T(8,128)} %all-reduce.5.cloned.1.call-done) | copy-start | bytes 786436
Sparse Core Ops, SparseCore 0:
  60.9 56.7 reduce-scatter.3
  156.1 32.3 all-reduce.4
  193.1 72.7 all-reduce.6
where the time goes:
time: 275 us; the launch traced here: 274 us
  waiting for transfers between devices  163 us (59%)
  blocking collectives  26.1 us (9%)
  starting transfers between devices  25.2 us (9%)
  local copies, waits for them, and re-layouts  22.1 us (8%)
  matrix products  18.5 us (7%)
  between operations  14.6 us (5%)
  other arithmetic  4.08 us (1%)
    unnamed x5, waiting for transfers between devices  76.3 us
    psum x1, waiting for transfers between devices, per_device(): kernel_block = lax.psum(2.0 * exchange_term - direct, 'ga')  32.5 us
    all_gather x1, blocking collectives, per_device(): lax.all_gather(pairs, 'ka', axis=0, tiled=True).reshape(n_ka, pair_rows, 3)  26.1 us
    all_to_all x1, waiting for transfers between devices, per_device(): lax.all_to_all(send_x, 'ka', split_axis=0, concat_axis=0, tiled=True)  19.6 us
    all_to_all x1, waiting for transfers between devices, per_device(): lax.all_to_all(send_p, 'ka', split_axis=0, concat_axis=0, tiled=True)  13.4 us
    all_to_all x1, waiting for transfers between devices, per_device(): lax.all_to_all(half_rows, 'ka', split_axis=1, concat_axis=1, tiled=True)  12 us
    all_to_all x1, waiting for transfers between devices, per_device(): lax.all_to_all(send_y, 'ka', split_axis=0, concat_axis=0, tiled=True)  9.42 us
    all_to_all x1, starting transfers between devices, per_device(): lax.all_to_all(send_q, 'ka', split_axis=0, concat_axis=0, tiled=True)  7.31 us
  transfers between devices with their start and end apart: 8, of which 8 were waited for; matrix products, arithmetic and copies ran while one was open for 7% of the time, Pallas kernels for 0%

commit v1 on v0

--- a/solution.py
+++ b/solution.py
@@ -60,7 +60,10 @@
         scatter_dimension=0,
         tiled=True,
     ).astype(jnp.bfloat16)
-    returned = lax.all_to_all(half_rows, "ka", split_axis=1, concat_axis=1, tiled=True)
+    size = lax.axis_size("ka")
+    pieces = jnp.stack(jnp.split(half_rows, size, axis=1), axis=0)
+    pieces = lax.all_to_all(pieces, "ka", split_axis=0, concat_axis=0)
+    returned = jnp.concatenate(pieces, axis=1)
     returned = returned.reshape(g_local, n_ka * CAPQ, transitions)
     u_rows = jnp.einsum(
         "js,gsi->jig", q_route, returned, preferred_element_type=jnp.float32

time: 275 us -> 292 us (1.062)
  local copies, waits for them, and re-layouts: 22.1 us -> 33.6 us
  waiting for transfers between devices: 163 us -> 169 us
    unnamed x5, waiting for transfers between devices: 76.3 us -> 93.9 us
    all_to_all x1, waiting for transfers between devices: 13.4 us -> 0.01 us  [per_device(): lax.all_to_all(send_p, 'ka', split_axis=0, concat_axis=0, tiled=True)]
    unnamed x20 -> x29, local copies, waits for them, and re-layouts: 3.49 us -> 12.7 us
  transfers between devices with their start and end apart: 8 -> 8, of which waited for: 8 -> 7; matrix products, arithmetic and copies ran while one was open for 7% -> 10% of each run, Pallas kernels for 0% -> 0%
where the time goes in v1:
time: 292 us; the launch traced here: 291 us
  waiting for transfers between devices  169 us (58%)
  local copies, waits for them, and re-layouts  33.6 us (12%)
  starting transfers between devices  26.5 us (9%)
  blocking collectives  26.1 us (9%)
  matrix products  18.5 us (6%)
  between operations  14.6 us (5%)
    unnamed x5, waiting for transfers between devices  93.9 us
    psum x1, waiting for transfers between devices, per_device(): kernel_block = lax.psum(2.0 * exchange_term - direct, 'ga')  31.5 us
    all_gather x1, blocking collectives, per_device(): lax.all_gather(pairs, 'ka', axis=0, tiled=True).reshape(n_ka, pair_rows, 3)  26.1 us
    all_to_all x1, waiting for transfers between devices, per_device(): lax.all_to_all(send_x, 'ka', split_axis=0, concat_axis=0, tiled=True)  19.6 us
    all_to_all x1, waiting for transfers between devices, per_device(): pieces = lax.all_to_all(pieces, 'ka', split_axis=0, concat_axis=0)  13.2 us
    unnamed x29, local copies, waits for them, and re-layouts  12.7 us
    all_to_all x1, waiting for transfers between devices, per_device(): lax.all_to_all(send_y, 'ka', split_axis=0, concat_axis=0, tiled=True)  11 us
    all_to_all x1, starting transfers between devices, per_device(): lax.all_to_all(send_q, 'ka', split_axis=0, concat_axis=0, tiled=True)  7.31 us
  transfers between devices with their start and end apart: 8, of which 7 were waited for; matrix products, arithmetic and copies ran while one was open for 10% of the time, Pallas kernels for 0%

profile of v1, /device:TPU:0, one launch (start us, length us, event | category | flops | bytes accessed | tf_op | source)
XLA Modules:
  0.0 291.2 jit_solution(9597512237130209519)
XLA Ops:
  9.9 7.3 %all-to-all-start.2 = ((s32[8,1,2]{2,1,0:T(1,128)}), s32[8,1,2]{2,1,0:T(1,128)S(1)}, u32[]{:S(2)}, u32[]{:S(2)}) async-start(s32[8,1,2]{2,1,0:T(1,128)} %bitcast.18), calls=%async_computation.2 | async-start | bytes 8192 | tf_op jit(solution)/shard_map/all_to_all | solution.py:50
  17.2 2.5 convolution_convert_fusion.3
  19.7 2.2 reshape.166
  23.6 5.8 %all-to-all-start.1 = ((bf16[8,2,64,375]{3,1,2,0:T(2,128)(2,1)}), bf16[8,2,64,375]{3,1,2,0:T(2,128)(2,1)S(1)}, u32[]{:S(2)}, u32[]{:S(2)}) async-start(bf16[8,2,64,375]{3,1,2,0:T(2,128)(2,1)} %copy.123), calls=%async_computation.1 | async-start | bytes 1572864 | tf_op jit(solution)/shard_map/all_to_all | solution.py:49
  29.5 19.6 %all-to-all-done.1 = bf16[8,2,64,375]{3,1,2,0:T(2,128)(2,1)S(1)} async-done(((bf16[8,2,64,375]{3,1,2,0:T(2,128)(2,1)}), bf16[8,2,64,375]{3,1,2,0:T(2,128)(2,1)S(1)}, u32[]{:S(2)}, u32[]{:S(2)}) %all-to-all-start.1) | async-done | bytes 768032 | tf_op jit(solution)/shard_map/all_to_all | solution.py:49
  49.2 4.9 %fusion = f32[8,2,64,1500,1]{3,2,4,1,0:T(8,128)} fusion(bf16[2,375,1500,1,1]{2,0,1,4,3:T(2,128)(2,1)S(1)} %bitcast.106, bf16[8,2,2]{2,1,0:T(2,128)(2,1)S(1)} %compare_convert_fusion, bf16[8,2,64,375]{3,2,1,0:T(8,128)(2,1)S(1)} %copy.124), kind=kOutput, calls=%fused_computation | convolution fusion | flops 2304768000 | bytes 9162064 | tf_op jit(solution)/shard_map/ncsig,sgh->hnci/dot_general | solution.py:54
  54.1 6.5 %copy.129 = f32[1500,8,128]{2,1,0:T(8,128)} copy(f32[1500,8,128]{0,2,1:T(8,128)} %bitcast.107) | data formatting | bytes 12288000 | tf_op jit(solution)/shard_map/reshape | solution.py:58
  61.3 26.1 %all-gather = s32[8,16,3]{1,2,0:T(4,128)S(1)} all-gather(s32[1,16,3]{1,2,0:T(4,128)S(1)} %bitcast.115), channel_id=1, replica_groups=mesh['ka'=8,'ga'=4] {'ka'}, dimensions={0}, use_global_device_ids=true | all-gather | bytes 1728 | tf_op jit(solution)/shard_map/all_gather | solution.py:71
  89.5 3.5 %all-to-all-start = ((bf16[8,2,64,375]{3,2,1,0:T(8,128)(2,1)}), bf16[8,2,64,375]{3,2,1,0:T(8,128)(2,1)S(1)}, u32[]{:S(2)}, u32[]{:S(2)}) async-start(bf16[8,2,64,375]{3,2,1,0:T(8,128)(2,1)} %copy.117), calls=%async_computation | async-start | bytes 1572864 | tf_op jit(solution)/shard_map/all_to_all | solution.py:90
  94.5 23.1 %reduce-scatter.4.cloned.1.call-done = f32[375,8,128]{2,1,0:T(8,128)} async-done(((f32[1500,8,128]{2,1,0:T(8,128)}), f32[375,8,128]{2,1,0:T(8,128)}) %reduce-scatter.4.cloned.1.call-update) | async-done | bytes 1536016
  117.6 1.7 copy.180
  120.8 5.5 %all-to-all-start.4 = ((bf16[8,2,64,375]{3,2,1,0:T(8,128)(2,1)}), bf16[8,2,64,375]{3,2,1,0:T(8,128)(2,1)}, u32[]{:S(2)}, u32[]{:S(2)}) async-start(bf16[8,2,64,375]{3,2,1,0:T(8,128)(2,1)} %copy.134), calls=%async_computation.4 | async-start | bytes 1572864 | tf_op jit(solution)/shard_map/all_to_all | solution.py:89
  129.4 1.5 fusion.27
  132.5 1.5 fusion.25
  134.0 1.5 fusion.24
  135.6 11.0 %all-to-all-done.4 = bf16[8,2,64,375]{3,2,1,0:T(8,128)(2,1)} async-done(((bf16[8,2,64,375]{3,2,1,0:T(8,128)(2,1)}), bf16[8,2,64,375]{3,2,1,0:T(8,128)(2,1)}, u32[]{:S(2)}, u32[]{:S(2)}) %all-to-all-start.4) | async-done | bytes 768032 | tf_op jit(solution)/shard_map/all_to_all | solution.py:89
  146.5 4.2 %all-to-all-start.3 = ((bf16[8,375,1,128]{3,1,2,0:T(8,128)(2,1)}), bf16[8,375,1,128]{3,1,2,0:T(8,128)(2,1)}, u32[]{:S(2)}, u32[]{:S(2)}) async-start(bf16[8,375,1,128]{3,1,2,0:T(8,128)(2,1)} %fusion.24), calls=%async_computation.3 | async-start | bytes 1540096 | tf_op jit(solution)/shard_map/all_to_all | solution.py:65
  152.1 2.6 convolution_convert_fusion
  154.7 2.3 fusion.6
  157.0 13.2 %all-to-all-done.3 = bf16[8,375,1,128]{3,1,2,0:T(8,128)(2,1)} async-done(((bf16[8,375,1,128]{3,1,2,0:T(8,128)(2,1)}), bf16[8,375,1,128]{3,1,2,0:T(8,128)(2,1)}, u32[]{:S(2)}, u32[]{:S(2)}) %all-to-all-start.3) | async-done | bytes 768032 | tf_op jit(solution)/shard_map/all_to_all | solution.py:65
  174.3 31.5 %all-reduce.5.cloned.1.call-done = f32[16,64,64]{2,1,0:T(8,128)} async-done(((f32[16,64,64]{2,1,0:T(8,128)}), f32[16,64,64]{2,1,0:T(8,128)}) %all-reduce.5.cloned.1.call-update) | async-done | bytes 262160 | tf_op jit(solution)/shard_map/psum | solution.py:113
  208.0 2.2 fusion.45
  212.4 70.8 %all-reduce.7.cloned.1.call-done = f32[32,4096]{1,0:T(8,128)} async-done(((f32[32,4096]{1,0:T(8,128)}), f32[32,4096]{1,0:T(8,128)}) %all-reduce.7.cloned.1.call-update) | async-done | bytes 524304
  283.2 1.5 constant_dynamic-slice_fusion
  (67 shorter events, 23.9 us)
Async XLA Ops:
  7.2 42.1 %copy-start = (bf16[2,375,1500]{2,0,1:T(2,128)(2,1)S(1)}, bf16[2,375,1500]{2,0,1:T(2,128)(2,1)}, u32[]{:S(2)}) copy-start(bf16[2,375,1500]{2,0,1:T(2,128)(2,1)} %param.11) | copy-start | bytes 6750004
  9.9 13.7 %all-to-all-start.2 = ((s32[8,1,2]{2,1,0:T(1,128)}), s32[8,1,2]{2,1,0:T(1,128)S(1)}, u32[]{:S(2)}, u32[]{:S(2)}) async-start(s32[8,1,2]{2,1,0:T(1,128)} %bitcast.18), calls=%async_computation.2 | async-start | bytes 8192 | tf_op jit(solution)/shard_map/all_to_all | solution.py:50
  23.6 25.5 %all-to-all-start.1 = ((bf16[8,2,64,375]{3,1,2,0:T(2,128)(2,1)}), bf16[8,2,64,375]{3,1,2,0:T(2,128)(2,1)S(1)}, u32[]{:S(2)}, u32[]{:S(2)}) async-start(bf16[8,2,64,375]{3,1,2,0:T(2,128)(2,1)} %copy.123), calls=%async_computation.1 | async-start | bytes 1572864 | tf_op jit(solution)/shard_map/all_to_all | solution.py:49
  29.4 88.2 %reduce-scatter.4.cloned.1.call-start = ((), (), s32[]{:S(2)}) async-start(), calls=%async_computation.8 | async-start | bytes 7680000
  60.6 0.7 copy-start.7
  60.6 27.4 %copy-start.5 = (bf16[4,64,375]{2,1,0:T(8,128)(2,1)S(1)}, bf16[4,64,375]{2,1,0:T(8,128)(2,1)}, u32[]{:S(2)}) copy-start(bf16[4,64,375]{2,1,0:T(8,128)(2,1)} %param.9) | copy-start | bytes 576004
  88.5 4.6 %copy-start.6 = (bf16[4,64,375]{2,1,0:T(8,128)(2,1)S(1)}, bf16[4,64,375]{2,1,0:T(8,128)(2,1)}, u32[]{:S(2)}) copy-start(bf16[4,64,375]{2,1,0:T(8,128)(2,1)} %param.8) | copy-start | bytes 576004
  89.5 31.4 %all-to-all-start = ((bf16[8,2,64,375]{3,2,1,0:T(8,128)(2,1)}), bf16[8,2,64,375]{3,2,1,0:T(8,128)(2,1)S(1)}, u32[]{:S(2)}, u32[]{:S(2)}) async-start(bf16[8,2,64,375]{3,2,1,0:T(8,128)(2,1)} %copy.117), calls=%async_computation | async-start | bytes 1572864 | tf_op jit(solution)/shard_map/all_to_all | solution.py:90
  119.3 0.9 copy-start.2
  120.8 25.7 %all-to-all-start.4 = ((bf16[8,2,64,375]{3,2,1,0:T(8,128)(2,1)}), bf16[8,2,64,375]{3,2,1,0:T(8,128)(2,1)}, u32[]{:S(2)}, u32[]{:S(2)}) async-start(bf16[8,2,64,375]{3,2,1,0:T(8,128)(2,1)} %copy.134), calls=%async_computation.4 | async-start | bytes 1572864 | tf_op jit(solution)/shard_map/all_to_all | solution.py:89
  126.4 24.6 %copy-start.8 = (f32[375]{0:T(512)S(1)}, f32[375]{0:T(512)}, u32[]{:S(2)}) copy-start(f32[375]{0:T(512)} %param.10) | copy-start | bytes 4504
  146.5 23.7 %all-to-all-start.3 = ((bf16[8,375,1,128]{3,1,2,0:T(8,128)(2,1)}), bf16[8,375,1,128]{3,1,2,0:T(8,128)(2,1)}, u32[]{:S(2)}, u32[]{:S(2)}) async-start(bf16[8,375,1,128]{3,1,2,0:T(8,128)(2,1)} %fusion.24), calls=%async_computation.3 | async-start | bytes 1540096 | tf_op jit(solution)/shard_map/all_to_all | solution.py:65
  150.8 55.0 %all-reduce.5.cloned.1.call-start = ((), (), s32[]{:S(2)}) async-start(), calls=%async_computation.6 | async-start | bytes 1048576 | tf_op jit(solution)/shard_map/psum | solution.py:113
  171.7 1.1 copy-start.1
  171.7 1.3 copy-start.4
  174.2 109.0 %all-reduce.7.cloned.1.call-start = ((), (), s32[]{:S(2)}) async-start(), calls=%async_computation.7 | async-start | bytes 1048576
  205.8 4.5 %copy-start.9 = (u32[32]{0:T(128)S(1)}, u32[32]{0:T(128)}, u32[]{:S(2)}) copy-start(u32[32]{0:T(128)} %constant.69) | copy-start | bytes 388
  205.8 5.7 %copy-start.3 = (f32[16,64,64]{2,1,0:T(8,128)S(1)}, f32[16,64,64]{2,1,0:T(8,128)}, u32[]{:S(2)}) copy-start(f32[16,64,64]{2,1,0:T(8,128)} %all-reduce.5.cloned.1.call-done) | copy-start | bytes 786436
Sparse Core Ops, SparseCore 0:
  60.8 56.7 reduce-scatter.3
  174.3 31.3 all-reduce.4
  210.4 72.7 all-reduce.6
